TPU v7x, 128 devices: a whole 4x4x4 slice. The times are simulated.
128 devices in a mesh: mp: 32 (over y, x, core), ffn: 4 (over z).
Axes of the slice: x: 4, y: 4, z: 4, core: 2. Of those that a mesh axis runs over, the one named last changes fastest.
Arguments:
- tokens: bfloat16 [512, 8192], P('ffn', 'mp'), may hold values from -6 to 6
- gate_weight: bfloat16 [8192, 28672], P('mp', 'ffn'), may hold values from -0.0625 to 0.0625
- up_weight: bfloat16 [8192, 28672], P('mp', 'ffn'), may hold values from -0.0625 to 0.0625
- down_weight: bfloat16 [28672, 8192], P('ffn', 'mp'), may hold values from -0.03125 to 0.03125
Outputs:
- mixed: bfloat16 [512, 8192], P('ffn', 'mp')
All inputs are finite; a program needn't handle non-finite values.
Results may differ from a plain program's by a relative error of at most 0.005.
Values may be sent and summed in bfloat16 or wider, within the bound.
A program may use at most 192 MiB of HBM per device.

v0:
```python
import jax
import jax.numpy as jnp
from jax import lax
from jax.experimental import pallas as pl
from jax.experimental.pallas import tpu as pltpu
from jax.sharding import PartitionSpec as P

MESH = pl.DeviceIdType.MESH
STREAMS = 4
LINKS = 4
ORDERS = ((0, 1, 3, 2), (1, 3, 2, 0), (1, 2, 3, 0), (2, 1, 3, 0))
F32 = jnp.float32
BF16 = jnp.bfloat16


def coded(v):
    return (v * jnp.abs(v)).astype(BF16)


def decoded(c):
    u = c.astype(F32)
    return u * lax.rsqrt(jnp.maximum(jnp.abs(u), 1e-37))


def kernel(
    tokens, gate, up, down, out,
    w, ws, dw, x, p, s1, r1, s2, r2, k2, s3, r3, k3, s4, r4, h, od, rd, t, tc, zr,
    ssem, rsem0, rsem, load_sem, tok_sem, relay_sem, w_sem, swap_sem, own_sem,
):
    rows, depth = tokens.shape
    units = w.shape[2]
    half, quarter = units // 2, units // 4
    sub = rows // LINKS
    part = sub // 2
    me = lax.axis_index("mp")
    z = lax.axis_index("ffn")
    core = lax.rem(me, 2)
    xpos = lax.rem(lax.div(me, 2), 4)
    ypos = lax.div(me, 8)
    sib = 1 - core
    sibling = me + 1 - 2 * core

    bits, peers = [], []
    for pos, stride in ((xpos, 2), (ypos, 8)):
        bits.append(lax.rem(lax.div(pos + 1, 2), 2))
        peers.append(me + stride * (1 - 2 * lax.rem(pos, 2)))
    for pos, stride in ((xpos, 2), (ypos, 8)):
        bits.append(lax.div(pos, 2))
        peers.append(me + stride * (lax.rem(pos + 1 + 2 * lax.rem(pos + 1, 2), 4) - pos))

    def bit(s, stage):
        return bits[(s + stage) % 4]

    def peer(s, stage):
        return peers[(s + stage) % 4]

    def along_z(j):
        return lax.rem(z + j, 4)

    def remote(src, dst, send, recv, mp, ffn):
        return pltpu.make_async_remote_copy(
            src_ref=src, dst_ref=dst, send_sem=send, recv_sem=recv,
            device_id={"mp": mp, "ffn": ffn}, device_id_type=MESH,
        )

    def lanes(start, size):
        return pl.ds(pl.multiple_of(start, 128), size)

    def sublanes(start, size):
        return pl.ds(pl.multiple_of(start, 16), size)

    mine, theirs = lanes(core * depth, depth), lanes(sib * depth, depth)
    my_rows = sublanes(core * depth, depth)

    pieces = [(0, 0), (1, 0), (0, 1), (1, 1)]
    token_load = pltpu.make_async_copy(tokens, x.at[0, :, mine], load_sem.at[0])
    token_load.start()
    stage_loads = []
    for i, (a, e) in enumerate(pieces):
        cols = pl.ds(a * half + e * quarter, quarter)
        from_cols = lanes(sib * units + a * half + e * quarter, quarter)
        for m, ref in enumerate((gate, up)):
            stage_loads.append(
                pltpu.make_async_copy(ref.at[:, from_cols], ws.at[m, :, cols], load_sem.at[1 + 2 * i + m]))
            stage_loads[-1].start()
        if i == 0:
            own_loads = []
            for m, ref in enumerate((gate, up)):
                own_loads.append(pltpu.make_async_copy(
                    ref.at[:, lanes(core * units, units)], w.at[m, my_rows, :], load_sem.at[9 + m]))
                own_loads[-1].start()
    down_load = pltpu.make_async_copy(
        down.at[sublanes(core * units, units), :], dw.at[:, mine], load_sem.at[11])
    down_load.start()

    barrier = pltpu.get_barrier_semaphore()
    partners = [(sibling, z)] + [(q, z) for q in peers] + [(me, along_z(j)) for j in range(1, 4)]
    for mp, ffn in partners:
        pl.semaphore_signal(barrier, inc=1, device_id={"mp": mp, "ffn": ffn}, device_id_type=MESH)
    with jax.named_scope("z_barrier"):
        pl.semaphore_wait(barrier, len(partners))

    def token_copy(j):
        return remote(
            x.at[0, :, mine], x.at[4 - j, :, mine], tok_sem.at[0, j], tok_sem.at[1, 4 - j], me, along_z(j))

    def relay_copy(j):
        block = x.at[j, :, mine]
        return remote(block, block, relay_sem.at[0, j], relay_sem.at[1, j], sibling, z)

    def weight_copy(i):
        a, e = pieces[i]
        cols = pl.ds(a * half + e * quarter, quarter)
        return remote(ws.at[:, :, cols], w.at[:, my_rows, cols], w_sem.at[0, i], w_sem.at[1, i], sibling, z)

    down_copy = remote(
        down.at[sublanes(sib * units, units), :], dw.at[:, mine], w_sem.at[0, 4], w_sem.at[1, 4], sibling, z)

    def send_weights(i):
        stage_loads[2 * i].wait()
        stage_loads[2 * i + 1].wait()
        weight_copy(i).start()

    token_load.wait()
    for j in (1, 3, 2):
        token_copy(j).start()
    relay_copy(0).start()
    send_weights(0)
    send_weights(1)

    def partial(j, i):
        a, e = pieces[i]
        cols = pl.ds(a * half + e * quarter, quarter)
        for m in range(2):
            p[j, 2 * a + e, m] = jnp.dot(x[j], w[m, :, cols], preferred_element_type=F32)

    def by_rows(count, body):
        def step(i, carry):
            body(lax.div(i, count), lax.rem(i, count) * 16)
            return carry

        lax.fori_loop(0, 2 * count, step, 0)

    def first_copy(j, e, s):
        rs = pl.ds(s * sub, sub)
        return remote(
            s1.at[j, e, :, rs, :], r1.at[j, e, :, rs, :], ssem.at[0], rsem0.at[j, 4 * e + s], peer(s, 0), z)

    def first(j, e):
        for s in range(LINKS):

            def body(m, at, s=s):
                rs = sublanes(s * sub + at, 16)
                s1[j, e, m, rs, :] = coded(p[j, 2 * (1 - bit(s, 0)) + e, m, rs, :])

            by_rows(sub // 16, body)
            first_copy(j, e, s).start()

    with jax.named_scope("z_load"):
        for load in own_loads:
            load.wait()
        relay_copy(0).wait_recv()
    with jax.named_scope("z_w0"):
        weight_copy(0).wait_recv()
    partial(0, 0)
    with jax.named_scope("z_tok"):
        for j in (1, 3):
            token_copy(4 - j).wait_recv()
            relay_copy(j).start()
    send_weights(2)
    with jax.named_scope("z_w1"):
        weight_copy(1).wait_recv()
    with jax.named_scope("z_f00"):
        partial(0, 1)
        first(0, 0)
    with jax.named_scope("z_rel1"):
        relay_copy(1).wait_recv()
    with jax.named_scope("z_f10"):
        partial(1, 0)
        partial(1, 1)
        first(1, 0)
    with jax.named_scope("z_tok2"):
        token_copy(2).wait_recv()
        relay_copy(2).start()
    send_weights(3)
    with jax.named_scope("z_w23"):
        weight_copy(2).wait_recv()
        partial(0, 2)
        partial(1, 2)
        weight_copy(3).wait_recv()
    with jax.named_scope("z_f01"):
        for j in (0, 1):
            partial(j, 3)
            first(j, 1)
    for j in (3, 2):
        with jax.named_scope("z_f%d" % j):
            relay_copy(j).wait_recv()
            for e in range(2):
                partial(j, 2 * e)
                partial(j, 2 * e + 1)
                first(j, e)
    down_copy.start()

    def second_copy(j, s):
        rs = pl.ds(s * sub, sub)
        return remote(s2.at[j, :, rs, :], r2.at[j, :, rs, :], ssem.at[1], rsem.at[0, j, s], peer(s, 1), z)

    def second(j):
        def add(dst, s, e, done):
            def body(m, at):
                rs = sublanes(s * sub + at, 16)
                dst[j, m, rs, :] = done(p[j, 2 * bit(s, 0) + e, m, rs, :] + decoded(r1[j, e, m, rs, :]))

            by_rows(sub // 16, body)

        for s in range(LINKS):
            for e in range(2):
                first_copy(j, e, s).wait_recv()
            add(s2, s, 1 - bit(s, 1), coded)
            second_copy(j, s).start()
        for s in range(LINKS):
            add(k2, s, bit(s, 1), lambda v: v)

    def third_copy(j, s):
        rs = pl.ds(s * part, part)
        return remote(s3.at[j, :, rs, :], r3.at[j, :, rs, :], ssem.at[2], rsem.at[1, j, s], peer(s, 2), z)

    def third(j):
        def add(dst, s, side, done):
            def body(m, at):
                rs = sublanes(s * part + at, 16)
                src = sublanes(s * sub + side * part + at, 16)
                dst[j, m, rs, :] = done(k2[j, m, src, :] + decoded(r2[j, m, src, :]))

            by_rows(part // 16, body)

        for s in range(LINKS):
            second_copy(j, s).wait_recv()
            add(s3, s, 1 - bit(s, 2), coded)
            third_copy(j, s).start()
        for s in range(LINKS):
            add(k3, s, bit(s, 2), lambda v: v)

    def fourth_copy(j, s):
        rs = pl.ds(s * part, part)
        return remote(s4.at[j, :, rs, :], r4.at[j, :, rs, :], ssem.at[3], rsem.at[2, j, s], peer(s, 3), z)

    def fourth(j):
        for s in range(LINKS):
            third_copy(j, s).wait_recv()

            def body(m, at, s=s):
                rs = sublanes(s * part + at, 16)
                v = k3[j, m, rs, :] + decoded(r3[j, m, rs, :])
                k3[j, m, rs, :] = v
                s4[j, m, rs, :] = coded(v)

            by_rows(part // 16, body)
            fourth_copy(j, s).start()

    def gather_copy(step, j, s):
        row, col = s * sub, bit(s, 0) * half
        n_rows, n_cols = sub, half
        if step < 2:
            col, n_cols = col + bit(s, 1) * quarter, quarter
        if step < 1:
            row, n_rows = row + bit(s, 2) * part, part
        block = h.at[j, sublanes(row, n_rows), lanes(col, n_cols)]
        return remote(block, block, ssem.at[4 + step], rsem.at[3 + step, j, s], peer(s, 2 - step), z)

    def hidden(j):
        for s in range(LINKS):
            fourth_copy(j, s).wait_recv()
            row, cols = s * sub + bit(s, 2) * part, lanes(bit(s, 0) * half + bit(s, 1) * quarter, quarter)

            def body(i, carry, s=s, row=row, cols=cols):
                rs = sublanes(s * part + i * 16, 16)
                g = k3[j, 0, rs, :] + decoded(r4[j, 0, rs, :])
                u = k3[j, 1, rs, :] + decoded(r4[j, 1, rs, :])
                value = g / (1.0 + jnp.exp(-g)) * u
                h[j, sublanes(row + i * 16, 16), cols] = value.astype(BF16)
                return carry

            lax.fori_loop(0, part // 16, body, 0)
            gather_copy(0, j, s).start()

    def gather(step, j):
        for s in range(LINKS):
            gather_copy(step - 1, j, s).wait_recv()
            gather_copy(step, j, s).start()

    def phase(name, order, run):
        for j in order:
            with jax.named_scope("z_%s%d" % (name, j)):
                run(j)

    phase("second", ORDERS[1], second)
    phase("third", ORDERS[2], third)
    phase("fourth", ORDERS[3], fourth)
    phase("hidden", ORDERS[3], hidden)
    phase("ga", ORDERS[3], lambda j: gather(1, j))
    phase("gb", ORDERS[3], lambda j: gather(2, j))

    down_load.wait()
    down_copy.wait_recv()

    def swap_copy(j):
        return remote(od.at[j], rd.at[j], swap_sem.at[0, j], swap_sem.at[1, j], sibling, z)

    def owner_copy(j):
        return remote(tc.at[j], zr.at[3 - j], own_sem.at[0, j], own_sem.at[1, 4 - j], me, along_z(j))

    def project(j):
        with jax.named_scope("z_gc%d" % j):
            for s in range(LINKS):
                gather_copy(2, j, s).wait_recv()
        with jax.named_scope("z_dot%d" % j):
            od[j] = jnp.dot(h[j], dw[:, theirs], preferred_element_type=F32)
            swap_copy(j).start()
            t[j] = jnp.dot(h[j], dw[:, mine], preferred_element_type=F32)

    def to_owner(j):
        with jax.named_scope("z_swap%d" % j):
            swap_copy(j).wait_recv()
        tc[j] = coded(t[j] + rd[j])
        owner_copy(j).start()

    last = None
    for j in ORDERS[3]:
        project(j)
        if last is not None:
            to_owner(last)
        last = j

    for j in range(1, 4):
        token_copy(j).wait_send()
        owner_copy(j).wait_send()
    for j in range(4):
        relay_copy(j).wait_send()
        weight_copy(j).wait_send()
    down_copy.wait_send()
    everything = [s1, s2, s3, s4, h.at[0, pl.ds(0, rows // 2), :], h.at[0], h.at[pl.ds(0, 2)]]
    for i, sent in enumerate(everything):
        remote(sent, sent, ssem.at[i], rsem.at[0, 0, 0], sibling, z).wait_send()
    for j in range(4):
        swap_copy(j).wait_send()
    with jax.named_scope("z_swap0"):
        swap_copy(0).wait_recv()
    with jax.named_scope("z_own"):
        for j in range(1, 4):
            owner_copy(j).wait_recv()
    total = t[0] + rd[0]
    for j in range(3):
        total += decoded(zr[j])
    out[...] = total.astype(out.dtype)


def local(tokens, gate, up, down):
    rows, depth = tokens.shape
    units = gate.shape[1] // 2
    quarter = units // 4
    sem = pltpu.SemaphoreType.DMA
    tall, low = (STREAMS, 2, rows, quarter), (STREAMS, 2, rows // 2, quarter)
    result = (STREAMS, rows, depth)
    return pl.pallas_call(
        kernel,
        out_shape=jax.ShapeDtypeStruct((rows, depth), BF16),
        in_specs=[pl.BlockSpec(memory_space=pl.ANY)] * 4,
        out_specs=pl.BlockSpec(memory_space=pltpu.VMEM),
        scratch_shapes=[
            pltpu.VMEM((2, 2 * depth, units), BF16),
            pltpu.VMEM((2, depth, units), BF16),
            pltpu.VMEM((units, 2 * depth), BF16),
            pltpu.VMEM((STREAMS, rows, 2 * depth), BF16),
            pltpu.VMEM((STREAMS, 4, 2, rows, quarter), F32),
            *[pltpu.VMEM((STREAMS, 2, 2, rows, quarter), BF16) for _ in range(2)],
            *[pltpu.VMEM(tall, dtype) for dtype in (BF16, BF16, F32)],
            *[pltpu.VMEM(low, dtype) for dtype in (BF16, BF16, F32)],
            *[pltpu.VMEM(low, dtype) for dtype in (BF16, BF16)],
            pltpu.VMEM((STREAMS, rows, units), BF16),
            pltpu.VMEM(result, F32),
            pltpu.VMEM(result, F32),
            pltpu.VMEM(result, F32),
            pltpu.VMEM(result, BF16),
            pltpu.VMEM((3, rows, depth), BF16),
            sem((7,)),
            sem((STREAMS, 2 * LINKS)),
            sem((6, STREAMS, LINKS)),
            sem((12,)),
            sem((2, STREAMS)),
            sem((2, STREAMS)),
            sem((2, 5)),
            sem((2, STREAMS)),
            sem((2, STREAMS)),
        ],
        compiler_params=pltpu.CompilerParams(
            collective_id=0, has_side_effects=True, vmem_limit_bytes=60 * 2**20
        ),
    )(tokens, gate, up, down)


def solution(mesh):
    placed = (P("ffn", "mp"), P("mp", "ffn"), P("mp", "ffn"), P("ffn", "mp"))
    return jax.shard_map(
        local, mesh=mesh, in_specs=placed, out_specs=P("ffn", "mp"), check_vma=False
    )
```

profile of v0, /device:TPU:1, one launch (start us, length us, event | category | flops | bytes accessed | tf_op | source)
XLA Modules:
  0.0 78.7 jit_solution(5742537933043893737)
XLA Ops:
  0.0 77.2 %shard_map.46 = bf16[128,256]{1,0:T(8,128)(2,1)} custom-call(bf16[128,256]{1,0:T(8,128)(2,1)} %tokens.1, bf16[256,7168]{1,0:T(8,128)(2,1)} %gate.1, bf16[256,7168]{1,0:T(8,128)(2,1)} %up.1, bf16[7168,256]{1,0:T(8,128)(2,1)} %down.1), custom_call_target="tpu_custom_call" | custom-call | tf_op jit(solution)/shard_map/pallas_call | solution.py:365
  77.2 1.5 %copy.6 = bf16[128,256]{1,0:T(8,128)(2,1)} copy(bf16[128,256]{1,0:T(8,128)(2,1)} %shard_map.46) | data formatting | bytes 131072
where the time goes:
time: 79.4 us; the launch traced here: 78.7 us
  Pallas kernels  77.2 us (97%)
  local copies, waits for them, and re-layouts  1.47 us (2%)
    pallas_call x1, Pallas kernels, local(): pl.pallas_call(kernel, out_shape=jax.ShapeDtypeStruct((rows, depth), BF16...  77.2 us

commit v1 on v0

--- a/solution.py
+++ b/solution.py
@@ -25,7 +25,7 @@
 def kernel(
     tokens, gate, up, down, out,
     w, ws, dw, x, p, s1, r1, s2, r2, k2, s3, r3, k3, s4, r4, h, od, rd, t, tc, zr,
-    ssem, rsem0, rsem, load_sem, tok_sem, relay_sem, w_sem, swap_sem, own_sem,
+    sx, rx, ssem, rsem0, rsem, load_sem, tok_sem, relay_sem, w_sem, sx_sem, swap_sem, own_sem,
 ):
     rows, depth = tokens.shape
     units = w.shape[2]
@@ -70,63 +70,92 @@
         return pl.ds(pl.multiple_of(start, 16), size)
 
     mine, theirs = lanes(core * depth, depth), lanes(sib * depth, depth)
-    my_rows = sublanes(core * depth, depth)
+    my_rows, their_rows = sublanes(core * depth, depth), sublanes(sib * depth, depth)
 
     pieces = [(0, 0), (1, 0), (0, 1), (1, 1)]
     token_load = pltpu.make_async_copy(tokens, x.at[0, :, mine], load_sem.at[0])
     token_load.start()
-    stage_loads = []
-    for i, (a, e) in enumerate(pieces):
+    for a, e in pieces:
         cols = pl.ds(a * half + e * quarter, quarter)
         from_cols = lanes(sib * units + a * half + e * quarter, quarter)
         for m, ref in enumerate((gate, up)):
-            stage_loads.append(
-                pltpu.make_async_copy(ref.at[:, from_cols], ws.at[m, :, cols], load_sem.at[1 + 2 * i + m]))
-            stage_loads[-1].start()
-        if i == 0:
-            own_loads = []
-            for m, ref in enumerate((gate, up)):
-                own_loads.append(pltpu.make_async_copy(
-                    ref.at[:, lanes(core * units, units)], w.at[m, my_rows, :], load_sem.at[9 + m]))
-                own_loads[-1].start()
+            pltpu.make_async_copy(ref.at[:, from_cols], ws.at[m, :, cols], load_sem.at[1 + e]).start()
+    own_loads = []
+    for m, ref in enumerate((gate, up)):
+        own_loads.append(pltpu.make_async_copy(
+            ref.at[:, lanes(core * units, units)], w.at[m, my_rows, :], load_sem.at[3 + m]))
+        own_loads[-1].start()
     down_load = pltpu.make_async_copy(
-        down.at[sublanes(core * units, units), :], dw.at[:, mine], load_sem.at[11])
+        down.at[sublanes(core * units, units), :], dw.at[:, mine], load_sem.at[5])
     down_load.start()
+
+    def wait_staged(e):
+        pltpu.make_async_copy(gate.at[:, pl.ds(0, units)], ws.at[0], load_sem.at[1 + e]).wait()
 
     barrier = pltpu.get_barrier_semaphore()
     partners = [(sibling, z)] + [(q, z) for q in peers] + [(me, along_z(j)) for j in range(1, 4)]
     for mp, ffn in partners:
         pl.semaphore_signal(barrier, inc=1, device_id={"mp": mp, "ffn": ffn}, device_id_type=MESH)
+
+    def by_rows(count, body):
+        def step(i, carry):
+            body(lax.div(i, count), lax.rem(i, count) * 16)
+            return carry
+
+        lax.fori_loop(0, 2 * count, step, 0)
+
+    def own_part(e):
+        wait_staged(e)
+        for a in range(2):
+            cols = pl.ds(a * half + e * quarter, quarter)
+            for m in range(2):
+                p[1, 2 * a + e, m] = jnp.dot(x[0, :, mine], ws[m, :, cols], preferred_element_type=F32)
+        for s in range(LINKS):
+
+            def body(m, at, s=s):
+                rs = sublanes(s * sub + at, 16)
+                sx[e, m, rs, :] = coded(p[1, 2 * (1 - bit(s, 0)) + e, m, rs, :])
+
+            by_rows(sub // 16, body)
+
+    with jax.named_scope("z_tload"):
+        token_load.wait()
+    with jax.named_scope("z_own0"):
+        own_part(0)
     with jax.named_scope("z_barrier"):
         pl.semaphore_wait(barrier, len(partners))
 
     def token_copy(j):
-        return remote(
-            x.at[0, :, mine], x.at[4 - j, :, mine], tok_sem.at[0, j], tok_sem.at[1, 4 - j], me, along_z(j))
+        return remote(x.at[0, :, mine], x.at[4 - j, :, mine], ssem.at[7], tok_sem.at[4 - j], me, along_z(j))
 
     def relay_copy(j):
         block = x.at[j, :, mine]
-        return remote(block, block, relay_sem.at[0, j], relay_sem.at[1, j], sibling, z)
+        return remote(block, block, ssem.at[8], relay_sem.at[j], sibling, z)
 
     def weight_copy(i):
         a, e = pieces[i]
         cols = pl.ds(a * half + e * quarter, quarter)
-        return remote(ws.at[:, :, cols], w.at[:, my_rows, cols], w_sem.at[0, i], w_sem.at[1, i], sibling, z)
+        return remote(ws.at[:, :, cols], w.at[:, my_rows, cols], ssem.at[9], w_sem.at[e], sibling, z)
+
+    def wait_weights(e):
+        block = ws.at[:, :, pl.ds(0, half)]
+        remote(block, block, ssem.at[9], w_sem.at[e], sibling, z).wait_recv()
 
     down_copy = remote(
-        down.at[sublanes(sib * units, units), :], dw.at[:, mine], w_sem.at[0, 4], w_sem.at[1, 4], sibling, z)
-
-    def send_weights(i):
-        stage_loads[2 * i].wait()
-        stage_loads[2 * i + 1].wait()
-        weight_copy(i).start()
-
-    token_load.wait()
+        down.at[sublanes(sib * units, units), :], dw.at[:, mine], ssem.at[10], w_sem.at[2], sibling, z)
+
+    def part_copy(e):
+        return remote(sx.at[e], rx.at[e], ssem.at[11], sx_sem.at[e], sibling, z)
+
     for j in (1, 3, 2):
         token_copy(j).start()
+    part_copy(0).start()
     relay_copy(0).start()
-    send_weights(0)
-    send_weights(1)
+    with jax.named_scope("z_own1"):
+        own_part(1)
+    part_copy(1).start()
+    weight_copy(0).start()
+    weight_copy(1).start()
 
     def partial(j, i):
         a, e = pieces[i]
@@ -134,17 +163,10 @@
         for m in range(2):
             p[j, 2 * a + e, m] = jnp.dot(x[j], w[m, :, cols], preferred_element_type=F32)
 
-    def by_rows(count, body):
-        def step(i, carry):
-            body(lax.div(i, count), lax.rem(i, count) * 16)
-            return carry
-
-        lax.fori_loop(0, 2 * count, step, 0)
-
     def first_copy(j, e, s):
         rs = pl.ds(s * sub, sub)
         return remote(
-            s1.at[j, e, :, rs, :], r1.at[j, e, :, rs, :], ssem.at[0], rsem0.at[j, 4 * e + s], peer(s, 0), z)
+            s1.at[j, e, :, rs, :], r1.at[j, e, :, rs, :], ssem.at[0], rsem0.at[j, e], peer(s, 0), z)
 
     def first(j, e):
         for s in range(LINKS):
@@ -156,23 +178,37 @@
             by_rows(sub // 16, body)
             first_copy(j, e, s).start()
 
+    def received(block, sem):
+        remote(block, block, ssem.at[0], sem, sibling, z).wait_recv()
+
     with jax.named_scope("z_load"):
         for load in own_loads:
             load.wait()
-        relay_copy(0).wait_recv()
-    with jax.named_scope("z_w0"):
-        weight_copy(0).wait_recv()
-    partial(0, 0)
+    with jax.named_scope("z_d0"):
+        for i in range(4):
+            a, e = pieces[i]
+            cols = pl.ds(a * half + e * quarter, quarter)
+            for m in range(2):
+                p[0, 2 * a + e, m] = jnp.dot(x[0, :, mine], w[m, my_rows, cols], preferred_element_type=F32)
+    for e in range(2):
+        with jax.named_scope("z_f0%d" % e):
+            part_copy(e).wait_recv()
+            for s in range(LINKS):
+
+                def body(m, at, s=s, e=e):
+                    rs = sublanes(s * sub + at, 16)
+                    own = p[0, 2 * (1 - bit(s, 0)) + e, m, rs, :]
+                    s1[0, e, m, rs, :] = coded(own + decoded(rx[e, m, rs, :]))
+
+                by_rows(sub // 16, body)
+                first_copy(0, e, s).start()
     with jax.named_scope("z_tok"):
         for j in (1, 3):
             token_copy(4 - j).wait_recv()
             relay_copy(j).start()
-    send_weights(2)
-    with jax.named_scope("z_w1"):
-        weight_copy(1).wait_recv()
-    with jax.named_scope("z_f00"):
-        partial(0, 1)
-        first(0, 0)
+    weight_copy(2).start()
+    with jax.named_scope("z_w0"):
+        wait_weights(0)
     with jax.named_scope("z_rel1"):
         relay_copy(1).wait_recv()
     with jax.named_scope("z_f10"):
@@ -182,16 +218,13 @@
     with jax.named_scope("z_tok2"):
         token_copy(2).wait_recv()
         relay_copy(2).start()
-    send_weights(3)
+    weight_copy(3).start()
     with jax.named_scope("z_w23"):
-        weight_copy(2).wait_recv()
-        partial(0, 2)
+        wait_weights(1)
+    with jax.named_scope("z_f11"):
         partial(1, 2)
-        weight_copy(3).wait_recv()
-    with jax.named_scope("z_f01"):
-        for j in (0, 1):
-            partial(j, 3)
-            first(j, 1)
+        partial(1, 3)
+        first(1, 1)
     for j in (3, 2):
         with jax.named_scope("z_f%d" % j):
             relay_copy(j).wait_recv()
@@ -201,9 +234,17 @@
                 first(j, e)
     down_copy.start()
 
+    with jax.named_scope("z_rest"):
+        relay_copy(0).wait_recv()
+        for a, e in pieces:
+            cols = pl.ds(a * half + e * quarter, quarter)
+            for m in range(2):
+                p[0, 2 * a + e, m] += jnp.dot(
+                    x[0, :, theirs], w[m, their_rows, cols], preferred_element_type=F32)
+
     def second_copy(j, s):
         rs = pl.ds(s * sub, sub)
-        return remote(s2.at[j, :, rs, :], r2.at[j, :, rs, :], ssem.at[1], rsem.at[0, j, s], peer(s, 1), z)
+        return remote(s2.at[j, :, rs, :], r2.at[j, :, rs, :], ssem.at[1], rsem.at[0, j], peer(s, 1), z)
 
     def second(j):
         def add(dst, s, e, done):
@@ -213,9 +254,9 @@
 
             by_rows(sub // 16, body)
 
-        for s in range(LINKS):
-            for e in range(2):
-                first_copy(j, e, s).wait_recv()
+        for e in range(2):
+            received(r1.at[j, e], rsem0.at[j, e])
+        for s in range(LINKS):
             add(s2, s, 1 - bit(s, 1), coded)
             second_copy(j, s).start()
         for s in range(LINKS):
@@ -223,7 +264,7 @@
 
     def third_copy(j, s):
         rs = pl.ds(s * part, part)
-        return remote(s3.at[j, :, rs, :], r3.at[j, :, rs, :], ssem.at[2], rsem.at[1, j, s], peer(s, 2), z)
+        return remote(s3.at[j, :, rs, :], r3.at[j, :, rs, :], ssem.at[2], rsem.at[1, j], peer(s, 2), z)
 
     def third(j):
         def add(dst, s, side, done):
@@ -234,8 +275,8 @@
 
             by_rows(part // 16, body)
 
-        for s in range(LINKS):
-            second_copy(j, s).wait_recv()
+        received(r2.at[j], rsem.at[0, j])
+        for s in range(LINKS):
             add(s3, s, 1 - bit(s, 2), coded)
             third_copy(j, s).start()
         for s in range(LINKS):
@@ -243,11 +284,11 @@
 
     def fourth_copy(j, s):
         rs = pl.ds(s * part, part)
-        return remote(s4.at[j, :, rs, :], r4.at[j, :, rs, :], ssem.at[3], rsem.at[2, j, s], peer(s, 3), z)
+        return remote(s4.at[j, :, rs, :], r4.at[j, :, rs, :], ssem.at[3], rsem.at[2, j], peer(s, 3), z)
 
     def fourth(j):
-        for s in range(LINKS):
-            third_copy(j, s).wait_recv()
+        received(r3.at[j], rsem.at[1, j])
+        for s in range(LINKS):
 
             def body(m, at, s=s):
                 rs = sublanes(s * part + at, 16)
@@ -266,11 +307,11 @@
         if step < 1:
             row, n_rows = row + bit(s, 2) * part, part
         block = h.at[j, sublanes(row, n_rows), lanes(col, n_cols)]
-        return remote(block, block, ssem.at[4 + step], rsem.at[3 + step, j, s], peer(s, 2 - step), z)
+        return remote(block, block, ssem.at[4 + step], rsem.at[3 + step, j], peer(s, 2 - step), z)
 
     def hidden(j):
-        for s in range(LINKS):
-            fourth_copy(j, s).wait_recv()
+        received(r4.at[j], rsem.at[2, j])
+        for s in range(LINKS):
             row, cols = s * sub + bit(s, 2) * part, lanes(bit(s, 0) * half + bit(s, 1) * quarter, quarter)
 
             def body(i, carry, s=s, row=row, cols=cols):
@@ -284,9 +325,13 @@
             lax.fori_loop(0, part // 16, body, 0)
             gather_copy(0, j, s).start()
 
+    def gathered(step, j):
+        size = (part, sub, 2 * sub)[step]
+        received(h.at[j, pl.ds(0, size), :], rsem.at[3 + step, j])
+
     def gather(step, j):
-        for s in range(LINKS):
-            gather_copy(step - 1, j, s).wait_recv()
+        gathered(step - 1, j)
+        for s in range(LINKS):
             gather_copy(step, j, s).start()
 
     def phase(name, order, run):
@@ -305,15 +350,14 @@
     down_copy.wait_recv()
 
     def swap_copy(j):
-        return remote(od.at[j], rd.at[j], swap_sem.at[0, j], swap_sem.at[1, j], sibling, z)
+        return remote(od.at[j], rd.at[j], ssem.at[12], swap_sem.at[j], sibling, z)
 
     def owner_copy(j):
-        return remote(tc.at[j], zr.at[3 - j], own_sem.at[0, j], own_sem.at[1, 4 - j], me, along_z(j))
+        return remote(tc.at[j], zr.at[3 - j], ssem.at[13], own_sem.at[4 - j], me, along_z(j))
 
     def project(j):
         with jax.named_scope("z_gc%d" % j):
-            for s in range(LINKS):
-                gather_copy(2, j, s).wait_recv()
+            gathered(2, j)
         with jax.named_scope("z_dot%d" % j):
             od[j] = jnp.dot(h[j], dw[:, theirs], preferred_element_type=F32)
             swap_copy(j).start()
@@ -325,30 +369,25 @@
         tc[j] = coded(t[j] + rd[j])
         owner_copy(j).start()
 
-    last = None
     for j in ORDERS[3]:
         project(j)
-        if last is not None:
-            to_owner(last)
-        last = j
-
-    for j in range(1, 4):
-        token_copy(j).wait_send()
-        owner_copy(j).wait_send()
-    for j in range(4):
-        relay_copy(j).wait_send()
-        weight_copy(j).wait_send()
+        if j:
+            to_owner(j)
+
+    for i, sent in enumerate((
+        s1, s2, s3, s4, h.at[0, pl.ds(0, rows // 2), :], h.at[0], h.at[pl.ds(0, 2)],
+        x.at[pl.ds(0, 3), :, mine], x.at[:, :, mine], ws, None, sx, od,
+    )):
+        if sent is not None:
+            remote(sent, sent, ssem.at[i], rsem.at[0, 0], sibling, z).wait_send()
     down_copy.wait_send()
-    everything = [s1, s2, s3, s4, h.at[0, pl.ds(0, rows // 2), :], h.at[0], h.at[pl.ds(0, 2)]]
-    for i, sent in enumerate(everything):
-        remote(sent, sent, ssem.at[i], rsem.at[0, 0, 0], sibling, z).wait_send()
-    for j in range(4):
-        swap_copy(j).wait_send()
     with jax.named_scope("z_swap0"):
         swap_copy(0).wait_recv()
     with jax.named_scope("z_own"):
         for j in range(1, 4):
             owner_copy(j).wait_recv()
+    sent = tc.at[pl.ds(0, 3)]
+    remote(sent, sent, ssem.at[13], rsem.at[0, 0], sibling, z).wait_send()
     total = t[0] + rd[0]
     for j in range(3):
         total += decoded(zr[j])
@@ -364,7 +403,7 @@
     result = (STREAMS, rows, depth)
     return pl.pallas_call(
         kernel,
-        out_shape=jax.ShapeDtypeStruct((rows, depth), BF16),
+        out_shape=pltpu.VMEM((rows, depth), BF16),
         in_specs=[pl.BlockSpec(memory_space=pl.ANY)] * 4,
         out_specs=pl.BlockSpec(memory_space=pltpu.VMEM),
         scratch_shapes=[
@@ -383,15 +422,17 @@
             pltpu.VMEM(result, F32),
             pltpu.VMEM(result, BF16),
             pltpu.VMEM((3, rows, depth), BF16),
-            sem((7,)),
-            sem((STREAMS, 2 * LINKS)),
-            sem((6, STREAMS, LINKS)),
-            sem((12,)),
-            sem((2, STREAMS)),
-            sem((2, STREAMS)),
-            sem((2, 5)),
-            sem((2, STREAMS)),
-            sem((2, STREAMS)),
+            *[pltpu.VMEM((2, 2, rows, quarter), BF16) for _ in range(2)],
+            sem((14,)),
+            sem((STREAMS, 2)),
+            sem((6, STREAMS)),
+            sem((6,)),
+            sem((STREAMS,)),
+            sem((STREAMS,)),
+            sem((3,)),
+            sem((2,)),
+            sem((STREAMS,)),
+            sem((STREAMS,)),
         ],
         compiler_params=pltpu.CompilerParams(
             collective_id=0, has_side_effects=True, vmem_limit_bytes=60 * 2**20

time: 79.4 us -> 75 us (0.945)
  Pallas kernels: 77.2 us -> 74.3 us
  local copies, waits for them, and re-layouts: 1.47 us -> 0.63 us
    pallas_call x1, Pallas kernels: 77.2 us -> 74.3 us  [local(): pl.pallas_call(kernel, out_shape=pltpu.VMEM((rows, depth), BF16), in_spec...]
    unnamed x1, local copies, waits for them, and re-layouts: 1.47 us -> 0.63 us
where the time goes in v1:
time: 75 us; the launch traced here: 74.9 us
  Pallas kernels  74.3 us (99%)
    pallas_call x1, Pallas kernels, local(): pl.pallas_call(kernel, out_shape=pltpu.VMEM((rows, depth), BF16), in_spec...  74.3 us

profile of v1, /device:TPU:1, one launch (start us, length us, event | category | flops | bytes accessed | tf_op | source)
XLA Modules:
  0.0 74.9 jit_solution(4425047367067087530)
XLA Ops:
  0.0 74.3 %shard_map.46 = bf16[128,256]{1,0:T(8,128)(2,1)S(1)} custom-call(bf16[128,256]{1,0:T(8,128)(2,1)} %tokens.1, bf16[256,7168]{1,0:T(8,128)(2,1)} %gate.1, bf16[256,7168]{1,0:T(8,128)(2,1)} %up.1, bf16[7168,256]{1,0:T(8,128)(2,1)} %down.1), custom_call_target="tpu_custom_call" | custom-call | tf_op jit(solution)/shard_map/pallas_call | solution.py:404
  74.3 0.6 copy.6

commit v2 on v1

--- a/solution.py
+++ b/solution.py
@@ -1,3 +1,6 @@
+import functools
+import itertools
+
 import jax
 import jax.numpy as jnp
 from jax import lax
@@ -8,9 +11,16 @@
 MESH = pl.DeviceIdType.MESH
 STREAMS = 4
 LINKS = 4
-ORDERS = ((0, 1, 3, 2), (1, 3, 2, 0), (1, 2, 3, 0), (2, 1, 3, 0))
+WAVE = (
+    (1, 1), (1, 3), (1, 2), (2, 1), (2, 3), (1, 0), (2, 2), (3, 1),
+    (3, 3), (2, 0), (3, 2), (4, 1), (4, 3), (3, 0), (4, 2), (5, 1),
+    (5, 3), (4, 0), (5, 2), (6, 1), (6, 2), (5, 0), (6, 3), (7, 1),
+    (8, 1), (7, 2), (6, 0), (8, 2), (7, 3), (8, 3), (7, 0),
+)
 F32 = jnp.float32
 BF16 = jnp.bfloat16
+
+PROJECTED = min(i for i, (step, _) in enumerate(WAVE) if step == 7)
 
 
 def coded(v):
@@ -72,56 +82,42 @@
     mine, theirs = lanes(core * depth, depth), lanes(sib * depth, depth)
     my_rows, their_rows = sublanes(core * depth, depth), sublanes(sib * depth, depth)
 
-    pieces = [(0, 0), (1, 0), (0, 1), (1, 1)]
-    token_load = pltpu.make_async_copy(tokens, x.at[0, :, mine], load_sem.at[0])
-    token_load.start()
-    for a, e in pieces:
-        cols = pl.ds(a * half + e * quarter, quarter)
-        from_cols = lanes(sib * units + a * half + e * quarter, quarter)
-        for m, ref in enumerate((gate, up)):
-            pltpu.make_async_copy(ref.at[:, from_cols], ws.at[m, :, cols], load_sem.at[1 + e]).start()
-    own_loads = []
-    for m, ref in enumerate((gate, up)):
-        own_loads.append(pltpu.make_async_copy(
-            ref.at[:, lanes(core * units, units)], w.at[m, my_rows, :], load_sem.at[3 + m]))
-        own_loads[-1].start()
-    down_load = pltpu.make_async_copy(
-        down.at[sublanes(core * units, units), :], dw.at[:, mine], load_sem.at[5])
-    down_load.start()
-
-    def wait_staged(e):
-        pltpu.make_async_copy(gate.at[:, pl.ds(0, units)], ws.at[0], load_sem.at[1 + e]).wait()
-
     barrier = pltpu.get_barrier_semaphore()
     partners = [(sibling, z)] + [(q, z) for q in peers] + [(me, along_z(j)) for j in range(1, 4)]
     for mp, ffn in partners:
         pl.semaphore_signal(barrier, inc=1, device_id={"mp": mp, "ffn": ffn}, device_id_type=MESH)
 
-    def by_rows(count, body):
-        def step(i, carry):
-            body(lax.div(i, count), lax.rem(i, count) * 16)
-            return carry
-
-        lax.fori_loop(0, 2 * count, step, 0)
-
-    def own_part(e):
-        wait_staged(e)
+    pieces = [(0, 0), (1, 0), (0, 1), (1, 1)]
+    token_load = pltpu.make_async_copy(tokens, x.at[0, :, mine], load_sem.at[8])
+    token_load.start()
+    for e, own, m in itertools.product(range(2), repeat=3):
+        ref = (gate, up)[m]
+        for a in range(2):
+            at = a * half + e * quarter
+            cols, from_cols = pl.ds(at, quarter), lanes((core if own else sib) * units + at, quarter)
+            dst = w.at[m, my_rows, cols] if own else ws.at[m, :, cols]
+            pltpu.make_async_copy(ref.at[:, from_cols], dst, load_sem.at[4 * e + 2 * own + m]).start()
+    down_load = pltpu.make_async_copy(
+        down.at[sublanes(core * units, units), :], dw.at[:, mine], load_sem.at[9])
+    down_load.start()
+
+    def wait_loaded(e, own, m):
+        pltpu.make_async_copy(
+            gate.at[:, pl.ds(0, half)], ws.at[0, :, pl.ds(0, half)], load_sem.at[4 * e + 2 * own + m]).wait()
+
+    def own_part(e, m):
+        wait_loaded(e, 0, m)
         for a in range(2):
             cols = pl.ds(a * half + e * quarter, quarter)
-            for m in range(2):
-                p[1, 2 * a + e, m] = jnp.dot(x[0, :, mine], ws[m, :, cols], preferred_element_type=F32)
-        for s in range(LINKS):
-
-            def body(m, at, s=s):
-                rs = sublanes(s * sub + at, 16)
-                sx[e, m, rs, :] = coded(p[1, 2 * (1 - bit(s, 0)) + e, m, rs, :])
-
-            by_rows(sub // 16, body)
+            p[1, 2 * a + e, m] = jnp.dot(x[0, :, mine], ws[m, :, cols], preferred_element_type=F32)
+        for s in range(LINKS):
+            rs = pl.ds(s * sub, sub)
+            sx[e, m, rs, :] = coded(p[1, 2 * (1 - bit(s, 0)) + e, m, rs, :])
 
     with jax.named_scope("z_tload"):
         token_load.wait()
     with jax.named_scope("z_own0"):
-        own_part(0)
+        own_part(0, 0)
     with jax.named_scope("z_barrier"):
         pl.semaphore_wait(barrier, len(partners))
 
@@ -144,18 +140,26 @@
     down_copy = remote(
         down.at[sublanes(sib * units, units), :], dw.at[:, mine], ssem.at[10], w_sem.at[2], sibling, z)
 
-    def part_copy(e):
-        return remote(sx.at[e], rx.at[e], ssem.at[11], sx_sem.at[e], sibling, z)
-
+    def part_copy(e, m):
+        return remote(sx.at[e, m], rx.at[e, m], ssem.at[11], sx_sem.at[2 * e + m], sibling, z)
+
+    def own_rows(e, m):
+        wait_loaded(e, 1, m)
+        for a in range(2):
+            cols = pl.ds(a * half + e * quarter, quarter)
+            p[0, 2 * a + e, m] = jnp.dot(x[0, :, mine], w[m, my_rows, cols], preferred_element_type=F32)
+
+    part_copy(0, 0).start()
     for j in (1, 3, 2):
         token_copy(j).start()
-    part_copy(0).start()
+    with jax.named_scope("z_own01"):
+        own_part(0, 1)
+        part_copy(0, 1).start()
     relay_copy(0).start()
-    with jax.named_scope("z_own1"):
-        own_part(1)
-    part_copy(1).start()
     weight_copy(0).start()
-    weight_copy(1).start()
+    with jax.named_scope("z_d0"):
+        for m in range(2):
+            own_rows(0, m)
 
     def partial(j, i):
         a, e = pieces[i]
@@ -168,45 +172,45 @@
         return remote(
             s1.at[j, e, :, rs, :], r1.at[j, e, :, rs, :], ssem.at[0], rsem0.at[j, e], peer(s, 0), z)
 
+    def half_copy(e, s, m):
+        rs = pl.ds(s * sub, sub)
+        return remote(
+            s1.at[0, e, m, rs, :], r1.at[0, e, m, rs, :], ssem.at[0], rsem0.at[0, e], peer(s, 0), z)
+
     def first(j, e):
         for s in range(LINKS):
 
-            def body(m, at, s=s):
-                rs = sublanes(s * sub + at, 16)
+            rs = pl.ds(s * sub, sub)
+            for m in range(2):
                 s1[j, e, m, rs, :] = coded(p[j, 2 * (1 - bit(s, 0)) + e, m, rs, :])
-
-            by_rows(sub // 16, body)
             first_copy(j, e, s).start()
 
     def received(block, sem):
         remote(block, block, ssem.at[0], sem, sibling, z).wait_recv()
 
-    with jax.named_scope("z_load"):
-        for load in own_loads:
-            load.wait()
-    with jax.named_scope("z_d0"):
-        for i in range(4):
-            a, e = pieces[i]
-            cols = pl.ds(a * half + e * quarter, quarter)
-            for m in range(2):
-                p[0, 2 * a + e, m] = jnp.dot(x[0, :, mine], w[m, my_rows, cols], preferred_element_type=F32)
     for e in range(2):
         with jax.named_scope("z_f0%d" % e):
-            part_copy(e).wait_recv()
-            for s in range(LINKS):
-
-                def body(m, at, s=s, e=e):
-                    rs = sublanes(s * sub + at, 16)
+            for m in range(2):
+                part_copy(e, m).wait_recv()
+                for s in range(LINKS):
+                    rs = pl.ds(s * sub, sub)
                     own = p[0, 2 * (1 - bit(s, 0)) + e, m, rs, :]
                     s1[0, e, m, rs, :] = coded(own + decoded(rx[e, m, rs, :]))
-
-                by_rows(sub // 16, body)
-                first_copy(0, e, s).start()
+                    half_copy(e, s, m).start()
+        if e == 0:
+            with jax.named_scope("z_own1"):
+                for m in range(2):
+                    own_part(1, m)
+                    part_copy(1, m).start()
+                weight_copy(1).start()
+                for m in range(2):
+                    own_rows(1, m)
     with jax.named_scope("z_tok"):
         for j in (1, 3):
             token_copy(4 - j).wait_recv()
             relay_copy(j).start()
     weight_copy(2).start()
+    weight_copy(3).start()
     with jax.named_scope("z_w0"):
         wait_weights(0)
     with jax.named_scope("z_rel1"):
@@ -218,9 +222,9 @@
     with jax.named_scope("z_tok2"):
         token_copy(2).wait_recv()
         relay_copy(2).start()
-    weight_copy(3).start()
     with jax.named_scope("z_w23"):
         wait_weights(1)
+    down_copy.start()
     with jax.named_scope("z_f11"):
         partial(1, 2)
         partial(1, 3)
@@ -232,7 +236,6 @@
                 partial(j, 2 * e)
                 partial(j, 2 * e + 1)
                 first(j, e)
-    down_copy.start()
 
     with jax.named_scope("z_rest"):
         relay_copy(0).wait_recv()
@@ -248,11 +251,9 @@
 
     def second(j):
         def add(dst, s, e, done):
-            def body(m, at):
-                rs = sublanes(s * sub + at, 16)
+            rs = pl.ds(s * sub, sub)
+            for m in range(2):
                 dst[j, m, rs, :] = done(p[j, 2 * bit(s, 0) + e, m, rs, :] + decoded(r1[j, e, m, rs, :]))
-
-            by_rows(sub // 16, body)
 
         for e in range(2):
             received(r1.at[j, e], rsem0.at[j, e])
@@ -268,12 +269,9 @@
 
     def third(j):
         def add(dst, s, side, done):
-            def body(m, at):
-                rs = sublanes(s * part + at, 16)
-                src = sublanes(s * sub + side * part + at, 16)
+            rs, src = pl.ds(s * part, part), sublanes(s * sub + side * part, part)
+            for m in range(2):
                 dst[j, m, rs, :] = done(k2[j, m, src, :] + decoded(r2[j, m, src, :]))
-
-            by_rows(part // 16, body)
 
         received(r2.at[j], rsem.at[0, j])
         for s in range(LINKS):
@@ -289,14 +287,11 @@
     def fourth(j):
         received(r3.at[j], rsem.at[1, j])
         for s in range(LINKS):
-
-            def body(m, at, s=s):
-                rs = sublanes(s * part + at, 16)
+            rs = pl.ds(s * part, part)
+            for m in range(2):
                 v = k3[j, m, rs, :] + decoded(r3[j, m, rs, :])
                 k3[j, m, rs, :] = v
                 s4[j, m, rs, :] = coded(v)
-
-            by_rows(part // 16, body)
             fourth_copy(j, s).start()
 
     def gather_copy(step, j, s):
@@ -313,16 +308,11 @@
         received(r4.at[j], rsem.at[2, j])
         for s in range(LINKS):
             row, cols = s * sub + bit(s, 2) * part, lanes(bit(s, 0) * half + bit(s, 1) * quarter, quarter)
-
-            def body(i, carry, s=s, row=row, cols=cols):
-                rs = sublanes(s * part + i * 16, 16)
-                g = k3[j, 0, rs, :] + decoded(r4[j, 0, rs, :])
-                u = k3[j, 1, rs, :] + decoded(r4[j, 1, rs, :])
-                value = g / (1.0 + jnp.exp(-g)) * u
-                h[j, sublanes(row + i * 16, 16), cols] = value.astype(BF16)
-                return carry
-
-            lax.fori_loop(0, part // 16, body, 0)
+            rs = pl.ds(s * part, part)
+            g = k3[j, 0, rs, :] + decoded(r4[j, 0, rs, :])
+            u = k3[j, 1, rs, :] + decoded(r4[j, 1, rs, :])
+            value = g / (1.0 + jnp.exp(-g)) * u
+            h[j, sublanes(row, part), cols] = value.astype(BF16)
             gather_copy(0, j, s).start()
 
     def gathered(step, j):
@@ -334,20 +324,6 @@
         for s in range(LINKS):
             gather_copy(step, j, s).start()
 
-    def phase(name, order, run):
-        for j in order:
-            with jax.named_scope("z_%s%d" % (name, j)):
-                run(j)
-
-    phase("second", ORDERS[1], second)
-    phase("third", ORDERS[2], third)
-    phase("fourth", ORDERS[3], fourth)
-    phase("hidden", ORDERS[3], hidden)
-    phase("ga", ORDERS[3], lambda j: gather(1, j))
-    phase("gb", ORDERS[3], lambda j: gather(2, j))
-
-    down_load.wait()
-    down_copy.wait_recv()
 
     def swap_copy(j):
         return remote(od.at[j], rd.at[j], ssem.at[12], swap_sem.at[j], sibling, z)
@@ -369,10 +345,15 @@
         tc[j] = coded(t[j] + rd[j])
         owner_copy(j).start()
 
-    for j in ORDERS[3]:
-        project(j)
-        if j:
-            to_owner(j)
+    steps = (
+        second, third, fourth, hidden, functools.partial(gather, 1), functools.partial(gather, 2), project, to_owner,
+    )
+    for i, (step, j) in enumerate(WAVE):
+        if i == PROJECTED:
+            down_load.wait()
+            down_copy.wait_recv()
+        with jax.named_scope("z_st%d_%d" % (step, j)):
+            steps[step - 1](j)
 
     for i, sent in enumerate((
         s1, s2, s3, s4, h.at[0, pl.ds(0, rows // 2), :], h.at[0], h.at[pl.ds(0, 2)],
@@ -426,11 +407,11 @@
             sem((14,)),
             sem((STREAMS, 2)),
             sem((6, STREAMS)),
-            sem((6,)),
+            sem((10,)),
             sem((STREAMS,)),
             sem((STREAMS,)),
             sem((3,)),
-            sem((2,)),
+            sem((4,)),
             sem((STREAMS,)),
             sem((STREAMS,)),
         ],

time: 75 us -> 73.2 us (0.976)
  Pallas kernels: 74.3 us -> 72.4 us
    pallas_call x1, Pallas kernels: 74.3 us -> 72.4 us  [local(): pl.pallas_call(kernel, out_shape=pltpu.VMEM((rows, depth), BF16), in_spec...]
where the time goes in v2:
time: 73.2 us; the launch traced here: 73.1 us
  Pallas kernels  72.4 us (99%)
    pallas_call x1, Pallas kernels, local(): pl.pallas_call(kernel, out_shape=pltpu.VMEM((rows, depth), BF16), in_spec...  72.4 us

profile of v2, /device:TPU:1, one launch (start us, length us, event | category | flops | bytes accessed | tf_op | source)
XLA Modules:
  0.0 73.1 jit_solution(13262727529295593752)
XLA Ops:
  0.0 72.4 %shard_map.46 = bf16[128,256]{1,0:T(8,128)(2,1)S(1)} custom-call(bf16[128,256]{1,0:T(8,128)(2,1)} %tokens.1, bf16[256,7168]{1,0:T(8,128)(2,1)} %gate.1, bf16[256,7168]{1,0:T(8,128)(2,1)} %up.1, bf16[7168,256]{1,0:T(8,128)(2,1)} %down.1), custom_call_target="tpu_custom_call" | custom-call | tf_op jit(solution)/shard_map/pallas_call | solution.py:385
  72.4 0.6 copy.6

commit v3 on v2

--- a/solution.py
+++ b/solution.py
@@ -122,7 +122,7 @@
         pl.semaphore_wait(barrier, len(partners))
 
     def token_copy(j):
-        return remote(x.at[0, :, mine], x.at[4 - j, :, mine], ssem.at[7], tok_sem.at[4 - j], me, along_z(j))
+        return remote(x.at[0, :, mine], x.at[4 - j, :, mine], ssem.at[7], tok_sem.at[3 - j], me, along_z(j))
 
     def relay_copy(j):
         block = x.at[j, :, mine]
@@ -170,12 +170,12 @@
     def first_copy(j, e, s):
         rs = pl.ds(s * sub, sub)
         return remote(
-            s1.at[j, e, :, rs, :], r1.at[j, e, :, rs, :], ssem.at[0], rsem0.at[j, e], peer(s, 0), z)
+            s1.at[j, e, :, rs, :], r1.at[j, e, :, rs, :], ssem.at[0], rsem0.at[j], peer(s, 0), z)
 
     def half_copy(e, s, m):
         rs = pl.ds(s * sub, sub)
         return remote(
-            s1.at[0, e, m, rs, :], r1.at[0, e, m, rs, :], ssem.at[0], rsem0.at[0, e], peer(s, 0), z)
+            s1.at[0, e, m, rs, :], r1.at[0, e, m, rs, :], ssem.at[0], rsem0.at[0], peer(s, 0), z)
 
     def first(j, e):
         for s in range(LINKS):
@@ -255,8 +255,7 @@
             for m in range(2):
                 dst[j, m, rs, :] = done(p[j, 2 * bit(s, 0) + e, m, rs, :] + decoded(r1[j, e, m, rs, :]))
 
-        for e in range(2):
-            received(r1.at[j, e], rsem0.at[j, e])
+        received(r1.at[j], rsem0.at[j])
         for s in range(LINKS):
             add(s2, s, 1 - bit(s, 1), coded)
             second_copy(j, s).start()
@@ -329,7 +328,7 @@
         return remote(od.at[j], rd.at[j], ssem.at[12], swap_sem.at[j], sibling, z)
 
     def owner_copy(j):
-        return remote(tc.at[j], zr.at[3 - j], ssem.at[13], own_sem.at[4 - j], me, along_z(j))
+        return remote(tc.at[j], zr.at[3 - j], ssem.at[13], own_sem.at[3 - j], me, along_z(j))
 
     def project(j):
         with jax.named_scope("z_gc%d" % j):
@@ -405,15 +404,15 @@
             pltpu.VMEM((3, rows, depth), BF16),
             *[pltpu.VMEM((2, 2, rows, quarter), BF16) for _ in range(2)],
             sem((14,)),
-            sem((STREAMS, 2)),
+            sem((STREAMS,)),
             sem((6, STREAMS)),
             sem((10,)),
-            sem((STREAMS,)),
+            sem((3,)),
             sem((STREAMS,)),
             sem((3,)),
             sem((4,)),
             sem((STREAMS,)),
-            sem((STREAMS,)),
+            sem((3,)),
         ],
         compiler_params=pltpu.CompilerParams(
             collective_id=0, has_side_effects=True, vmem_limit_bytes=60 * 2**20

time: 73.2 us -> 73.1 us (level)
  no operation moved by 1% of the time
where the time goes in v3:
time: 73.1 us; the launch traced here: 73 us
  Pallas kernels  72.4 us (99%)
    pallas_call x1, Pallas kernels, local(): pl.pallas_call(kernel, out_shape=pltpu.VMEM((rows, depth), BF16), in_spec...  72.4 us

profile of v3, /device:TPU:1, one launch (start us, length us, event | category | flops | bytes accessed | tf_op | source)
XLA Modules:
  0.0 73.0 jit_solution(1338122916034203470)
XLA Ops:
  0.0 72.4 %shard_map.46 = bf16[128,256]{1,0:T(8,128)(2,1)S(1)} custom-call(bf16[128,256]{1,0:T(8,128)(2,1)} %tokens.1, bf16[256,7168]{1,0:T(8,128)(2,1)} %gate.1, bf16[256,7168]{1,0:T(8,128)(2,1)} %up.1, bf16[7168,256]{1,0:T(8,128)(2,1)} %down.1), custom_call_target="tpu_custom_call" | custom-call | tf_op jit(solution)/shard_map/pallas_call | solution.py:384
  72.4 0.6 copy.6
